TPU v7x, 32 devices: a whole 2x2x4 slice. The times are simulated.
32 devices in a mesh: row: 8 (over z, y), col: 4 (over x, core).
Axes of the slice: x: 2, y: 2, z: 4, core: 2. Of those that a mesh axis runs over, the one named last changes fastest.
Arguments:
- matrix: float32 [4096, 4096], P('row', 'col'), may hold values from -0.92 to 1.92, as said below
Outputs:
- inverse: float32 [4096, 4096], P('row', 'col')
- residual_norms: float32 [4], replicated
Inputs may be any that keep to these rules, and one draw needn't show every extreme that they name: matrix is exactly symmetric and positive definite; all its eigenvalues lie between 0.08 and 1.92.
All inputs are finite; a program needn't handle non-finite values.
Results may differ from a plain program's by a relative error of at most 0.0017.
The roundings to bfloat16 on the way count: a program that leaves them out, or rounds other values in their place, can miss the bound.
Values may be sent and summed in bfloat16 or wider, within the bound.
A program may use at most 64 MiB of HBM per device.

v0:
```python
import jax
import jax.numpy as jnp
from jax import lax
from jax.sharding import PartitionSpec as P

N = 4096
ITERS = 4


def shards(matrix):
    row_count, col_count = matrix.shape
    row_index = lax.axis_index("row")
    col_index = lax.axis_index("col")
    sq_total = lax.psum(jnp.sum(matrix * matrix), ("row", "col"))
    start_scale = jnp.sqrt(jnp.float32(N)) / jnp.sqrt(sq_total)
    global_rows = row_index * row_count + lax.broadcasted_iota(jnp.int32, (row_count, col_count), 0)
    global_cols = col_index * col_count + lax.broadcasted_iota(jnp.int32, (row_count, col_count), 1)
    eye_block = (global_rows == global_cols).astype(jnp.float32)
    mat_low = matrix.astype(jnp.bfloat16)
    panel_rows = lax.all_gather(mat_low, "col", axis=1, tiled=True)
    current = start_scale * eye_block
    partial_list = []
    for iteration in range(ITERS):
        cur_low = current.astype(jnp.bfloat16)
        product = jnp.dot(
            panel_rows,
            lax.all_gather(cur_low, "row", axis=0, tiled=True),
            preferred_element_type=jnp.float32,
        )
        residual = eye_block - product
        local_sum = jnp.sum(residual * residual)
        partial_list.append(local_sum)
        shift_low = (eye_block + residual).astype(jnp.bfloat16)
        iterate_rows = lax.all_gather(cur_low, "col", axis=1, tiled=True)
        current = jnp.dot(
            iterate_rows,
            lax.all_gather(shift_low, "row", axis=0, tiled=True),
            preferred_element_type=jnp.float32,
        )
    summed = lax.psum(jnp.stack(partial_list), ("row", "col"))
    residual_norms = jnp.sqrt(summed / N)
    return (current, residual_norms)


def solution(mesh):
    in_specs = (P("row", "col"),)
    out_specs = (P("row", "col"), P())
    return jax.shard_map(shards, mesh=mesh, in_specs=in_specs, out_specs=out_specs, check_vma=False)
```

profile of v0, /device:TPU:0, one launch (start us, length us, event | category | flops | bytes accessed | tf_op | source)
XLA Modules:
  0.0 1244.2 jit_solution(14768718448786911574)
XLA Ops:
  7.2 4.3 fusion.5
  11.6 42.5 %psum.14 = f32[]{:T(128)} all-reduce(f32[]{:T(128)} %get-tuple-element.8), channel_id=1, replica_groups=mesh['row'=8,'col'=4] {'row','col'}, use_global_device_ids=true, to_apply=%region_1.0 | all-reduce | flops 1 | bytes 8 | tf_op jit(solution)/shard_map/psum | solution.py:14
  54.8 1.2 fusion
  56.9 124.6 %all-gather.16.cloned.1.call-done = bf16[4096,1024]{0,1:T(8,128)(2,1)} async-done(((bf16[512,1024]{0,1:T(8,128)(2,1)}), bf16[4096,1024]{0,1:T(8,128)(2,1)}) %all-gather.16.cloned.1.call-update) | async-done | bytes 8388624 | tf_op jit(solution)/shard_map/all_gather | solution.py:27
  181.5 10.1 fusion.1
  191.7 24.1 %all-gather.14.cloned.1.call-done = bf16[512,4096]{0,1:T(8,128)(2,1)} async-done(((bf16[512,1024]{0,1:T(8,128)(2,1)}), bf16[512,4096]{0,1:T(8,128)(2,1)}) %all-gather.14.cloned.1.call-update) | async-done | bytes 4194320 | tf_op jit(solution)/shard_map/all_gather | solution.py:34
  215.7 127.4 %all-gather.20.cloned.1.call-done = bf16[4096,1024]{0,1:T(8,128)(2,1)} async-done(((bf16[512,1024]{0,1:T(8,128)(2,1)}), bf16[4096,1024]{0,1:T(8,128)(2,1)}) %all-gather.20.cloned.1.call-update) | async-done | bytes 8388624 | tf_op jit(solution)/shard_map/all_gather | solution.py:37
  343.2 10.2 convolution_convert_fusion.2
  354.5 121.7 %all-gather.24.cloned.1.call-done = bf16[4096,1024]{1,0:T(8,128)(2,1)} async-done(((bf16[512,1024]{1,0:T(8,128)(2,1)}), bf16[4096,1024]{1,0:T(8,128)(2,1)}) %all-gather.24.cloned.1.call-update) | async-done | bytes 8388624 | tf_op jit(solution)/shard_map/all_gather | solution.py:27
  476.2 10.9 fusion.2
  487.1 23.1 %all-gather.22.cloned.1.call-done = bf16[512,4096]{1,0:T(8,128)(2,1)} async-done(((bf16[512,1024]{1,0:T(8,128)(2,1)}), bf16[512,4096]{1,0:T(8,128)(2,1)}) %all-gather.22.cloned.1.call-update) | async-done | bytes 4194320 | tf_op jit(solution)/shard_map/all_gather | solution.py:34
  510.3 127.0 %all-gather.26.cloned.1.call-done = bf16[4096,1024]{0,1:T(8,128)(2,1)} async-done(((bf16[512,1024]{0,1:T(8,128)(2,1)}), bf16[4096,1024]{0,1:T(8,128)(2,1)}) %all-gather.26.cloned.1.call-update) | async-done | bytes 8388624 | tf_op jit(solution)/shard_map/all_gather | solution.py:37
  637.3 10.2 convolution_convert_fusion.1
  648.4 121.9 %all-gather.30.cloned.1.call-done = bf16[4096,1024]{1,0:T(8,128)(2,1)} async-done(((bf16[512,1024]{1,0:T(8,128)(2,1)}), bf16[4096,1024]{1,0:T(8,128)(2,1)}) %all-gather.30.cloned.1.call-update) | async-done | bytes 8388624 | tf_op jit(solution)/shard_map/all_gather | solution.py:27
  770.3 10.9 fusion.3
  781.2 23.3 %all-gather.28.cloned.1.call-done = bf16[512,4096]{1,0:T(8,128)(2,1)} async-done(((bf16[512,1024]{1,0:T(8,128)(2,1)}), bf16[512,4096]{1,0:T(8,128)(2,1)}) %all-gather.28.cloned.1.call-update) | async-done | bytes 4194320 | tf_op jit(solution)/shard_map/all_gather | solution.py:34
  804.5 126.9 %all-gather.32.cloned.1.call-done = bf16[4096,1024]{0,1:T(8,128)(2,1)} async-done(((bf16[512,1024]{0,1:T(8,128)(2,1)}), bf16[4096,1024]{0,1:T(8,128)(2,1)}) %all-gather.32.cloned.1.call-update) | async-done | bytes 8388624 | tf_op jit(solution)/shard_map/all_gather | solution.py:37
  931.4 10.2 convolution_convert_fusion
  942.4 122.0 %all-gather.36.cloned.1.call-done = bf16[4096,1024]{1,0:T(8,128)(2,1)} async-done(((bf16[512,1024]{1,0:T(8,128)(2,1)}), bf16[4096,1024]{1,0:T(8,128)(2,1)}) %all-gather.36.cloned.1.call-update) | async-done | bytes 8388624 | tf_op jit(solution)/shard_map/all_gather | solution.py:27
  1064.4 12.9 %multiply_reduce_fusion.3 = (f32[]{:T(128)}, f32[]{:T(128)}, f32[]{:T(128)}, f32[]{:T(128)}, bf16[512,1024]{0,1:T(8,128)(2,1)}) fusion(f32[1024,512]{1,0:T(8,128)S(1)} %get-tuple-element.10, s32[512]{0:T(512)S(1)} %iota_add_fusion.1, s32[1024]{0:T(1024)S(1)} %iota_add_fusion, f32[1024,512]{1,0:T(8,128)} %get-tuple-element.12, ...), kind=kOutput, calls=%fused_computation.17 | convolution fusion | flops 4303355904 | bytes 19929104 | tf_op jit(solution)/shard_map/dot_general | solution.py:25
  1077.4 2.6 pad_maximum_fusion
  1079.9 39.1 %psum.15 = f32[4]{0:T(128)S(1)} all-reduce(f32[4]{0:T(128)S(1)} %pad_maximum_fusion), channel_id=1, replica_groups=mesh['row'=8,'col'=4] {'row','col'}, use_global_device_ids=true, to_apply=%region_6.0 | all-reduce | flops 4 | bytes 32 | tf_op jit(solution)/shard_map/psum | solution.py:40
  1119.6 107.3 %all-gather.38.cloned.1.call-done = bf16[4096,1024]{0,1:T(8,128)(2,1)} async-done(((bf16[512,1024]{0,1:T(8,128)(2,1)}), bf16[4096,1024]{0,1:T(8,128)(2,1)}) %all-gather.38.cloned.1.call-update) | async-done | bytes 8388624 | tf_op jit(solution)/shard_map/all_gather | solution.py:37
  1226.9 10.5 fusion.6
  (31 shorter events, 4.5 us)
Async XLA Ops:
  7.2 49.7 %all-gather.18.cloned.1.call-start = ((), (), s32[]{:S(2)}) async-start(), calls=%async_computation.2 | async-start | bytes 5242880 | tf_op jit(solution)/shard_map/all_gather | solution.py:20
  11.5 170.0 %all-gather.16.cloned.1.call-start = ((), (), s32[]{:S(2)}) async-start(), calls=%async_computation.1 | async-start | bytes 9437184 | tf_op jit(solution)/shard_map/all_gather | solution.py:27
  56.1 159.7 %all-gather.14.cloned.1.call-start = ((), (), s32[]{:S(2)}) async-start(), calls=%async_computation | async-start | bytes 5242880 | tf_op jit(solution)/shard_map/all_gather | solution.py:34
  56.8 286.4 %all-gather.20.cloned.1.call-start = ((), (), s32[]{:S(2)}) async-start(), calls=%async_computation.3 | async-start | bytes 9437184 | tf_op jit(solution)/shard_map/all_gather | solution.py:37
  191.6 284.6 %all-gather.24.cloned.1.call-start = ((), (), s32[]{:S(2)}) async-start(), calls=%async_computation.5 | async-start | bytes 9437184 | tf_op jit(solution)/shard_map/all_gather | solution.py:27
  353.4 156.9 %all-gather.22.cloned.1.call-start = ((), (), s32[]{:S(2)}) async-start(), calls=%async_computation.4 | async-start | bytes 5242880 | tf_op jit(solution)/shard_map/all_gather | solution.py:34
  354.0 283.3 %all-gather.26.cloned.1.call-start = ((), (), s32[]{:S(2)}) async-start(), calls=%async_computation.6 | async-start | bytes 9437184 | tf_op jit(solution)/shard_map/all_gather | solution.py:37
  487.1 283.2 %all-gather.30.cloned.1.call-start = ((), (), s32[]{:S(2)}) async-start(), calls=%async_computation.8 | async-start | bytes 9437184 | tf_op jit(solution)/shard_map/all_gather | solution.py:27
  647.5 157.0 %all-gather.28.cloned.1.call-start = ((), (), s32[]{:S(2)}) async-start(), calls=%async_computation.7 | async-start | bytes 5242880 | tf_op jit(solution)/shard_map/all_gather | solution.py:34
  648.2 283.2 %all-gather.32.cloned.1.call-start = ((), (), s32[]{:S(2)}) async-start(), calls=%async_computation.9 | async-start | bytes 9437184 | tf_op jit(solution)/shard_map/all_gather | solution.py:37
  781.2 283.2 %all-gather.36.cloned.1.call-start = ((), (), s32[]{:S(2)}) async-start(), calls=%async_computation.11 | async-start | bytes 9437184 | tf_op jit(solution)/shard_map/all_gather | solution.py:27
  941.6 178.0 %all-gather.34.cloned.1.call-start = ((), (), s32[]{:S(2)}) async-start(), calls=%async_computation.10 | async-start | bytes 5242880 | tf_op jit(solution)/shard_map/all_gather | solution.py:34
  942.2 284.7 %all-gather.38.cloned.1.call-start = ((), (), s32[]{:S(2)}) async-start(), calls=%async_computation.12 | async-start | bytes 9437184 | tf_op jit(solution)/shard_map/all_gather | solution.py:37
Sparse Core Ops, SparseCore 0:
  11.6 37.4 all-gather.17
  56.2 125.2 all-gather.15
  183.1 32.6 all-gather.13
  218.2 124.9 all-gather.19
  353.5 122.6 all-gather.23
  477.6 32.6 all-gather.21
  512.3 124.9 all-gather.25
  647.6 122.6 all-gather.29
  771.9 32.6 all-gather.27
  806.4 124.9 all-gather.31
  941.7 122.6 all-gather.35
  1065.8 33.3 all-gather.33
  1101.2 125.6 all-gather.37
where the time goes:
time: 1250 us; the launch traced here: 1240 us
  waiting for transfers between devices  1050 us (84%)
  matrix products  85.8 us (7%)
  blocking collectives  81.7 us (7%)
  between operations  14.9 us (1%)
    all_gather x4, waiting for transfers between devices, shards(): lax.all_gather(cur_low, 'row', axis=0, tiled=True)  490 us
    all_gather x4, waiting for transfers between devices, shards(): lax.all_gather(shift_low, 'row', axis=0, tiled=True)  489 us
    all_gather x4, waiting for transfers between devices, shards(): iterate_rows = lax.all_gather(cur_low, 'col', axis=1, tiled=True)  70.5 us
    dot_general x4, matrix products, shards(): jnp.dot(panel_rows, lax.all_gather(cur_low, 'row', axis=0, tiled=True), p...  44.8 us
    psum x1, blocking collectives, shards(): sq_total = lax.psum(jnp.sum(matrix * matrix), ('row', 'col'))  42.5 us
    dot_general x4, matrix products, shards(): jnp.dot(iterate_rows, lax.all_gather(shift_low, 'row', axis=0, tiled=True...  41 us
    psum x1, blocking collectives, shards(): summed = lax.psum(jnp.stack(partial_list), ('row', 'col'))  39.1 us
  transfers between devices with their start and end apart: 13, of which 11 were waited for; matrix products, arithmetic and copies ran while one was open for 4% of the time, Pallas kernels for 0%

commit v1 on v0

--- a/solution.py
+++ b/solution.py
@@ -31,7 +31,14 @@
         local_sum = jnp.sum(residual * residual)
         partial_list.append(local_sum)
         shift_low = (eye_block + residual).astype(jnp.bfloat16)
-        iterate_rows = lax.all_gather(cur_low, "col", axis=1, tiled=True)
+        ring = [cur_low]
+        for hop in range(3):
+            ring.append(lax.ppermute(ring[-1], "col", [(dev, (dev + 1) % 4) for dev in range(4)]))
+        iterate_rows = jnp.roll(
+            jnp.concatenate(ring[::-1], axis=1),
+            (lax.axis_index("col") + 1) * ring[0].shape[1],
+            axis=1,
+        )
         current = jnp.dot(
             iterate_rows,
             lax.all_gather(shift_low, "row", axis=0, tiled=True),

time: 1250 us -> 1170 us (0.936)
  waiting for transfers between devices: 1050 us -> 926 us
  matrix products: 85.8 us -> 110 us
  blocking collectives: 81.7 us -> 99 us
    all_gather x4, waiting for transfers between devices: 489 us -> 276 us  [shards(): lax.all_gather(shift_low, 'row', axis=0, tiled=True)]
    ppermute x0 -> x12, waiting for transfers between devices: none -> 157 us  [shards(): lax.ppermute(ring[-1], 'col', [(dev, (dev + 1) % 4) for dev in range(4)])]
    all_gather x4 -> x0, waiting for transfers between devices: 70.5 us -> none  [shards(): iterate_rows = lax.all_gather(cur_low, 'col', axis=1, tiled=True)]
    dot_general x4, matrix products: 41 us -> 64 us  [shards(): jnp.dot(iterate_rows, lax.all_gather(shift_low, 'row', axis=0, tiled=True...]
    psum x1, blocking collectives: 39.1 us -> 56.5 us  [shards(): summed = lax.psum(jnp.stack(partial_list), ('row', 'col'))]
  transfers between devices with their start and end apart: 13 -> 21, of which waited for: 11 -> 19; matrix products, arithmetic and copies ran while one was open for 4% -> 0% of each run, Pallas kernels for 0% -> 0%
where the time goes in v1:
time: 1170 us; the launch traced here: 1160 us
  waiting for transfers between devices  926 us (79%)
  matrix products  110 us (9%)
  blocking collectives  99 us (8%)
  between operations  15.3 us (1%)
    all_gather x4, waiting for transfers between devices, shards(): lax.all_gather(cur_low, 'row', axis=0, tiled=True)  493 us
    all_gather x4, waiting for transfers between devices, shards(): lax.all_gather(shift_low, 'row', axis=0, tiled=True)  276 us
    ppermute x12, waiting for transfers between devices, shards(): lax.ppermute(ring[-1], 'col', [(dev, (dev + 1) % 4) for dev in range(4)])  157 us
    dot_general x4, matrix products, shards(): jnp.dot(iterate_rows, lax.all_gather(shift_low, 'row', axis=0, tiled=True...  64 us
    psum x1, blocking collectives, shards(): summed = lax.psum(jnp.stack(partial_list), ('row', 'col'))  56.5 us
    dot_general x4, matrix products, shards(): jnp.dot(panel_rows, lax.all_gather(cur_low, 'row', axis=0, tiled=True), p...  45.9 us
    psum x1, blocking collectives, shards(): sq_total = lax.psum(jnp.sum(matrix * matrix), ('row', 'col'))  42.5 us
  transfers between devices with their start and end apart: 21, of which 19 were waited for; matrix products, arithmetic and copies ran while one was open for 0% of the time, Pallas kernels for 0%

profile of v1, /device:TPU:0, one launch (start us, length us, event | category | flops | bytes accessed | tf_op | source)
XLA Modules:
  0.0 1160.9 jit_solution(14153085332242222172)
XLA Ops:
  11.6 42.5 %psum.14 = f32[]{:T(128)} all-reduce(f32[]{:T(128)} %get-tuple-element.9), channel_id=1, replica_groups=mesh['row'=8,'col'=4] {'row','col'}, use_global_device_ids=true, to_apply=%region_1.0 | all-reduce | flops 1 | bytes 8 | tf_op jit(solution)/shard_map/psum | solution.py:14
  56.2 125.3 %all-gather.10.cloned.1.call-done = bf16[4096,1024]{0,1:T(8,128)(2,1)} async-done(((bf16[512,1024]{0,1:T(8,128)(2,1)}), bf16[4096,1024]{0,1:T(8,128)(2,1)}) %all-gather.10.cloned.1.call-update) | async-done | bytes 8388624 | tf_op jit(solution)/shard_map/all_gather | solution.py:27
  192.4 14.2 %collective-permute-done = bf16[512,1024]{0,1:T(8,128)(2,1)S(1)} collective-permute-done((bf16[512,1024]{0,1:T(8,128)(2,1)S(1)}, bf16[512,1024]{0,1:T(8,128)(2,1)S(1)}, u32[]{:S(2)}, u32[]{:S(2)}) %collective-permute-start) | collective-permute-done | bytes 1048608 | tf_op jit(solution)/shard_map/ppermute | solution.py:36
  206.6 14.2 %collective-permute-done.1 = bf16[512,1024]{0,1:T(8,128)(2,1)S(1)} collective-permute-done((bf16[512,1024]{0,1:T(8,128)(2,1)S(1)}, bf16[512,1024]{0,1:T(8,128)(2,1)S(1)}, u32[]{:S(2)}, u32[]{:S(2)}) %collective-permute-start.1) | collective-permute-done | bytes 1048608 | tf_op jit(solution)/shard_map/ppermute | solution.py:36
  221.1 14.3 %collective-permute-done.2 = bf16[512,1024]{0,1:T(8,128)(2,1)} collective-permute-done((bf16[512,1024]{0,1:T(8,128)(2,1)S(1)}, bf16[512,1024]{0,1:T(8,128)(2,1)}, u32[]{:S(2)}, u32[]{:S(2)}) %collective-permute-start.2) | collective-permute-done | bytes 1048608 | tf_op jit(solution)/shard_map/ppermute | solution.py:36
  235.4 80.2 %all-gather.14.cloned.1.call-done = bf16[4096,1024]{0,1:T(8,128)(2,1)} async-done(((bf16[512,1024]{0,1:T(8,128)(2,1)}), bf16[4096,1024]{0,1:T(8,128)(2,1)}) %all-gather.14.cloned.1.call-update) | async-done | bytes 8388624 | tf_op jit(solution)/shard_map/all_gather | solution.py:44
  315.6 24.7 %fusion.45 = bf16[512,1024]{1,0:T(8,128)(2,1)} fusion(bf16[4096,1024]{0,1:T(8,128)(2,1)} %all-gather.14.cloned.1.call-done, s32[]{:T(128)S(6)} %select_n.17, bf16[512,1024]{0,1:T(8,128)(2,1)} %collective-permute-done.2, bf16[512,1024]{0,1:T(8,128)(2,1)S(1)} %collective-permute-done.1, bf16[512,1024]{0,1:T(8,128)(2,1)S(1)} %collective-permute-done, ...), kind=kOutput, calls=%fused_computation.83 | convolution fusion | flops 4329046016 | bytes 13631492 | tf_op jit(solution)/shard_map/dot_general | solution.py:42
  340.4 122.8 %all-gather.16.cloned.1.call-done = bf16[4096,1024]{1,0:T(8,128)(2,1)} async-done(((bf16[512,1024]{1,0:T(8,128)(2,1)}), bf16[4096,1024]{1,0:T(8,128)(2,1)}) %all-gather.16.cloned.1.call-update) | async-done | bytes 8388624 | tf_op jit(solution)/shard_map/all_gather | solution.py:27
  474.2 14.2 %collective-permute-done.3 = bf16[512,1024]{1,0:T(8,128)(2,1)S(1)} collective-permute-done((bf16[512,1024]{1,0:T(8,128)(2,1)S(1)}, bf16[512,1024]{1,0:T(8,128)(2,1)S(1)}, u32[]{:S(2)}, u32[]{:S(2)}) %collective-permute-start.3) | collective-permute-done | bytes 1048608 | tf_op jit(solution)/shard_map/ppermute | solution.py:36
  488.4 14.2 %collective-permute-done.4 = bf16[512,1024]{1,0:T(8,128)(2,1)S(1)} collective-permute-done((bf16[512,1024]{1,0:T(8,128)(2,1)S(1)}, bf16[512,1024]{1,0:T(8,128)(2,1)S(1)}, u32[]{:S(2)}, u32[]{:S(2)}) %collective-permute-start.4) | collective-permute-done | bytes 1048608 | tf_op jit(solution)/shard_map/ppermute | solution.py:36
  502.8 14.3 %collective-permute-done.5 = bf16[512,1024]{1,0:T(8,128)(2,1)} collective-permute-done((bf16[512,1024]{1,0:T(8,128)(2,1)S(1)}, bf16[512,1024]{1,0:T(8,128)(2,1)}, u32[]{:S(2)}, u32[]{:S(2)}) %collective-permute-start.5) | collective-permute-done | bytes 1048608 | tf_op jit(solution)/shard_map/ppermute | solution.py:36
  517.1 80.2 %all-gather.18.cloned.1.call-done = bf16[4096,1024]{0,1:T(8,128)(2,1)} async-done(((bf16[512,1024]{0,1:T(8,128)(2,1)}), bf16[4096,1024]{0,1:T(8,128)(2,1)}) %all-gather.18.cloned.1.call-update) | async-done | bytes 8388624 | tf_op jit(solution)/shard_map/all_gather | solution.py:44
  610.6 122.5 %all-gather.20.cloned.1.call-done = bf16[4096,1024]{1,0:T(8,128)(2,1)} async-done(((bf16[512,1024]{1,0:T(8,128)(2,1)}), bf16[4096,1024]{1,0:T(8,128)(2,1)}) %all-gather.20.cloned.1.call-update) | async-done | bytes 8388624 | tf_op jit(solution)/shard_map/all_gather | solution.py:27
  744.2 14.2 %collective-permute-done.6 = bf16[512,1024]{1,0:T(8,128)(2,1)S(1)} collective-permute-done((bf16[512,1024]{1,0:T(8,128)(2,1)S(1)}, bf16[512,1024]{1,0:T(8,128)(2,1)S(1)}, u32[]{:S(2)}, u32[]{:S(2)}) %collective-permute-start.6) | collective-permute-done | bytes 1048608 | tf_op jit(solution)/shard_map/ppermute | solution.py:36
  758.4 14.2 %collective-permute-done.7 = bf16[512,1024]{1,0:T(8,128)(2,1)S(1)} collective-permute-done((bf16[512,1024]{1,0:T(8,128)(2,1)S(1)}, bf16[512,1024]{1,0:T(8,128)(2,1)S(1)}, u32[]{:S(2)}, u32[]{:S(2)}) %collective-permute-start.7) | collective-permute-done | bytes 1048608 | tf_op jit(solution)/shard_map/ppermute | solution.py:36
  772.8 14.3 %collective-permute-done.8 = bf16[512,1024]{1,0:T(8,128)(2,1)} collective-permute-done((bf16[512,1024]{1,0:T(8,128)(2,1)S(1)}, bf16[512,1024]{1,0:T(8,128)(2,1)}, u32[]{:S(2)}, u32[]{:S(2)}) %collective-permute-start.8) | collective-permute-done | bytes 1048608 | tf_op jit(solution)/shard_map/ppermute | solution.py:36
  787.1 80.2 %all-gather.22.cloned.1.call-done = bf16[4096,1024]{0,1:T(8,128)(2,1)} async-done(((bf16[512,1024]{0,1:T(8,128)(2,1)}), bf16[4096,1024]{0,1:T(8,128)(2,1)}) %all-gather.22.cloned.1.call-update) | async-done | bytes 8388624 | tf_op jit(solution)/shard_map/all_gather | solution.py:44
  880.6 122.5 %all-gather.24.cloned.1.call-done = bf16[4096,1024]{1,0:T(8,128)(2,1)} async-done(((bf16[512,1024]{1,0:T(8,128)(2,1)}), bf16[4096,1024]{1,0:T(8,128)(2,1)}) %all-gather.24.cloned.1.call-update) | async-done | bytes 8388624 | tf_op jit(solution)/shard_map/all_gather | solution.py:27
  1003.1 13.4 %multiply_reduce_fusion.3 = (f32[]{:T(128)}, f32[]{:T(128)}, f32[]{:T(128)}, f32[]{:T(128)}, bf16[512,1024]{0,1:T(8,128)(2,1)}) fusion(f32[1024,512]{1,0:T(8,128)} %get-tuple-element.11, s32[512]{0:T(512)S(1)} %iota_add_fusion.1, s32[1024]{0:T(1024)S(1)} %iota_add_fusion, f32[1024,512]{1,0:T(8,128)} %get-tuple-element.13, ...), kind=kOutput, calls=%fused_computation.81 | convolution fusion | flops 4303355904 | bytes 19929104 | tf_op jit(solution)/shard_map/dot_general | solution.py:25
  1016.6 14.2 %collective-permute-done.9 = bf16[512,1024]{1,0:T(8,128)(2,1)S(1)} collective-permute-done((bf16[512,1024]{1,0:T(8,128)(2,1)S(1)}, bf16[512,1024]{1,0:T(8,128)(2,1)S(1)}, u32[]{:S(2)}, u32[]{:S(2)}) %collective-permute-start.9) | collective-permute-done | bytes 1048608 | tf_op jit(solution)/shard_map/ppermute | solution.py:36
  1030.8 14.2 %collective-permute-done.10 = bf16[512,1024]{1,0:T(8,128)(2,1)S(1)} collective-permute-done((bf16[512,1024]{1,0:T(8,128)(2,1)S(1)}, bf16[512,1024]{1,0:T(8,128)(2,1)S(1)}, u32[]{:S(2)}, u32[]{:S(2)}) %collective-permute-start.10) | collective-permute-done | bytes 1048608 | tf_op jit(solution)/shard_map/ppermute | solution.py:36
  1047.7 56.5 %psum.15 = f32[4]{0:T(128)S(1)} all-reduce(f32[4]{0:T(128)S(1)} %pad_maximum_fusion), channel_id=1, replica_groups=mesh['row'=8,'col'=4] {'row','col'}, use_global_device_ids=true, to_apply=%region_6.8 | all-reduce | flops 4 | bytes 32 | tf_op jit(solution)/shard_map/psum | solution.py:47
  1104.7 35.8 %all-gather.26.cloned.1.call-done = bf16[4096,1024]{0,1:T(8,128)(2,1)} async-done(((bf16[512,1024]{0,1:T(8,128)(2,1)}), bf16[4096,1024]{0,1:T(8,128)(2,1)}) %all-gather.26.cloned.1.call-update) | async-done | bytes 8388624 | tf_op jit(solution)/shard_map/all_gather | solution.py:44
  1140.5 13.3 %fusion.4 = f32[512,1024]{1,0:T(8,128)} fusion(bf16[4096,1024]{0,1:T(8,128)(2,1)} %all-gather.26.cloned.1.call-done, s32[]{:T(128)S(6)} %select_n.17, bf16[512,1024]{1,0:T(8,128)(2,1)} %collective-permute-done.11, bf16[512,1024]{1,0:T(8,128)(2,1)S(1)} %collective-permute-done.10, bf16[512,1024]{1,0:T(8,128)(2,1)S(1)} %collective-permute-done.9, ...), kind=kOutput, calls=%fused_computation.45 | convolution fusion | flops 4328521728 | bytes 14680068 | tf_op jit(solution)/shard_map/dot_general | solution.py:42
  (51 shorter events, 69.1 us)
Async XLA Ops:
  7.2 49.0 %all-gather.12.cloned.1.call-start = ((), (), s32[]{:S(2)}) async-start(), calls=%async_computation.1 | async-start | bytes 5242880 | tf_op jit(solution)/shard_map/all_gather | solution.py:20
  11.5 170.0 %all-gather.10.cloned.1.call-start = ((), (), s32[]{:S(2)}) async-start(), calls=%async_computation | async-start | bytes 9437184 | tf_op jit(solution)/shard_map/all_gather | solution.py:27
  56.1 136.2 %copy-start = (bf16[512,1024]{0,1:T(8,128)(2,1)S(1)}, bf16[512,1024]{0,1:T(8,128)(2,1)}, u32[]{:S(2)}) copy-start(bf16[512,1024]{0,1:T(8,128)(2,1)} %fusion.40) | copy-start | bytes 3145732
  56.1 259.4 %all-gather.14.cloned.1.call-start = ((), (), s32[]{:S(2)}) async-start(), calls=%async_computation.2 | async-start | bytes 9437184 | tf_op jit(solution)/shard_map/all_gather | solution.py:44
  192.3 270.9 %all-gather.16.cloned.1.call-start = ((), (), s32[]{:S(2)}) async-start(), calls=%async_computation.3 | async-start | bytes 9437184 | tf_op jit(solution)/shard_map/all_gather | solution.py:27
  192.3 14.3 %collective-permute-start = (bf16[512,1024]{0,1:T(8,128)(2,1)S(1)}, bf16[512,1024]{0,1:T(8,128)(2,1)S(1)}, u32[]{:S(2)}, u32[]{:S(2)}) collective-permute-start(bf16[512,1024]{0,1:T(8,128)(2,1)S(1)} %copy-done), channel_id=1, source_target_pairs={{0,1},{1,2},{2,3},{3,0},{4,5},{5,6},{6,7},{7,4},{8,9},{9,10},{10,1... | collective-permute-start | bytes 3145736 | tf_op jit(solution)/shard_map/ppermute | solution.py:36
  206.6 14.2 %collective-permute-start.1 = (bf16[512,1024]{0,1:T(8,128)(2,1)S(1)}, bf16[512,1024]{0,1:T(8,128)(2,1)S(1)}, u32[]{:S(2)}, u32[]{:S(2)}) collective-permute-start(bf16[512,1024]{0,1:T(8,128)(2,1)S(1)} %collective-permute-done), channel_id=1, source_target_pairs={{0,1},{1,2},{2,3},{3,0},{4,5},{5,6},{6,7},{7,4},{8,9},{9,10},{10,1... | collective-permute-start | bytes 3145736 | tf_op jit(solution)/shard_map/ppermute | solution.py:36
  220.8 14.5 %collective-permute-start.2 = (bf16[512,1024]{0,1:T(8,128)(2,1)S(1)}, bf16[512,1024]{0,1:T(8,128)(2,1)}, u32[]{:S(2)}, u32[]{:S(2)}) collective-permute-start(bf16[512,1024]{0,1:T(8,128)(2,1)S(1)} %collective-permute-done.1), channel_id=1, source_target_pairs={{0,1},{1,2},{2,3},{3,0},{4,5},{5,6},{6,7},{7,4},{8,9},{9,10},{10,1... | collective-permute-start | bytes 3145736 | tf_op jit(solution)/shard_map/ppermute | solution.py:36
  340.3 133.8 %copy-start.2 = (bf16[512,1024]{1,0:T(8,128)(2,1)S(1)}, bf16[512,1024]{1,0:T(8,128)(2,1)}, u32[]{:S(2)}) copy-start(bf16[512,1024]{1,0:T(8,128)(2,1)} %fusion.45) | copy-start | bytes 3145732
  340.3 257.0 %all-gather.18.cloned.1.call-start = ((), (), s32[]{:S(2)}) async-start(), calls=%async_computation.4 | async-start | bytes 9437184 | tf_op jit(solution)/shard_map/all_gather | solution.py:44
  474.0 259.1 %all-gather.20.cloned.1.call-start = ((), (), s32[]{:S(2)}) async-start(), calls=%async_computation.5 | async-start | bytes 9437184 | tf_op jit(solution)/shard_map/all_gather | solution.py:27
  474.1 14.3 %collective-permute-start.3 = (bf16[512,1024]{1,0:T(8,128)(2,1)S(1)}, bf16[512,1024]{1,0:T(8,128)(2,1)S(1)}, u32[]{:S(2)}, u32[]{:S(2)}) collective-permute-start(bf16[512,1024]{1,0:T(8,128)(2,1)S(1)} %copy-done.2), channel_id=1, source_target_pairs={{0,1},{1,2},{2,3},{3,0},{4,5},{5,6},{6,7},{7,4},{8,9},{9,10},{10,1... | collective-permute-start | bytes 3145736 | tf_op jit(solution)/shard_map/ppermute | solution.py:36
  488.4 14.2 %collective-permute-start.4 = (bf16[512,1024]{1,0:T(8,128)(2,1)S(1)}, bf16[512,1024]{1,0:T(8,128)(2,1)S(1)}, u32[]{:S(2)}, u32[]{:S(2)}) collective-permute-start(bf16[512,1024]{1,0:T(8,128)(2,1)S(1)} %collective-permute-done.3), channel_id=1, source_target_pairs={{0,1},{1,2},{2,3},{3,0},{4,5},{5,6},{6,7},{7,4},{8,9},{9,10},{10,1... | collective-permute-start | bytes 3145736 | tf_op jit(solution)/shard_map/ppermute | solution.py:36
  502.6 14.5 %collective-permute-start.5 = (bf16[512,1024]{1,0:T(8,128)(2,1)S(1)}, bf16[512,1024]{1,0:T(8,128)(2,1)}, u32[]{:S(2)}, u32[]{:S(2)}) collective-permute-start(bf16[512,1024]{1,0:T(8,128)(2,1)S(1)} %collective-permute-done.4), channel_id=1, source_target_pairs={{0,1},{1,2},{2,3},{3,0},{4,5},{5,6},{6,7},{7,4},{8,9},{9,10},{10,1... | collective-permute-start | bytes 3145736 | tf_op jit(solution)/shard_map/ppermute | solution.py:36
  610.3 133.8 %copy-start.3 = (bf16[512,1024]{1,0:T(8,128)(2,1)S(1)}, bf16[512,1024]{1,0:T(8,128)(2,1)}, u32[]{:S(2)}) copy-start(bf16[512,1024]{1,0:T(8,128)(2,1)} %fusion.48) | copy-start | bytes 3145732
  610.3 257.0 %all-gather.22.cloned.1.call-start = ((), (), s32[]{:S(2)}) async-start(), calls=%async_computation.6 | async-start | bytes 9437184 | tf_op jit(solution)/shard_map/all_gather | solution.py:44
  744.0 259.1 %all-gather.24.cloned.1.call-start = ((), (), s32[]{:S(2)}) async-start(), calls=%async_computation.7 | async-start | bytes 9437184 | tf_op jit(solution)/shard_map/all_gather | solution.py:27
  744.1 14.3 %collective-permute-start.6 = (bf16[512,1024]{1,0:T(8,128)(2,1)S(1)}, bf16[512,1024]{1,0:T(8,128)(2,1)S(1)}, u32[]{:S(2)}, u32[]{:S(2)}) collective-permute-start(bf16[512,1024]{1,0:T(8,128)(2,1)S(1)} %copy-done.3), channel_id=1, source_target_pairs={{0,1},{1,2},{2,3},{3,0},{4,5},{5,6},{6,7},{7,4},{8,9},{9,10},{10,1... | collective-permute-start | bytes 3145736 | tf_op jit(solution)/shard_map/ppermute | solution.py:36
  758.4 14.2 %collective-permute-start.7 = (bf16[512,1024]{1,0:T(8,128)(2,1)S(1)}, bf16[512,1024]{1,0:T(8,128)(2,1)S(1)}, u32[]{:S(2)}, u32[]{:S(2)}) collective-permute-start(bf16[512,1024]{1,0:T(8,128)(2,1)S(1)} %collective-permute-done.6), channel_id=1, source_target_pairs={{0,1},{1,2},{2,3},{3,0},{4,5},{5,6},{6,7},{7,4},{8,9},{9,10},{10,1... | collective-permute-start | bytes 3145736 | tf_op jit(solution)/shard_map/ppermute | solution.py:36
  772.6 14.6 %collective-permute-start.8 = (bf16[512,1024]{1,0:T(8,128)(2,1)S(1)}, bf16[512,1024]{1,0:T(8,128)(2,1)}, u32[]{:S(2)}, u32[]{:S(2)}) collective-permute-start(bf16[512,1024]{1,0:T(8,128)(2,1)S(1)} %collective-permute-done.7), channel_id=1, source_target_pairs={{0,1},{1,2},{2,3},{3,0},{4,5},{5,6},{6,7},{7,4},{8,9},{9,10},{10,1... | collective-permute-start | bytes 3145736 | tf_op jit(solution)/shard_map/ppermute | solution.py:36
  880.3 260.2 %all-gather.26.cloned.1.call-start = ((), (), s32[]{:S(2)}) async-start(), calls=%async_computation.8 | async-start | bytes 9437184 | tf_op jit(solution)/shard_map/all_gather | solution.py:44
  1016.5 14.3 %collective-permute-start.9 = (bf16[512,1024]{1,0:T(8,128)(2,1)S(1)}, bf16[512,1024]{1,0:T(8,128)(2,1)S(1)}, u32[]{:S(2)}, u32[]{:S(2)}) collective-permute-start(bf16[512,1024]{1,0:T(8,128)(2,1)S(1)} %copy-done.1), channel_id=1, source_target_pairs={{0,1},{1,2},{2,3},{3,0},{4,5},{5,6},{6,7},{7,4},{8,9},{9,10},{10,1... | collective-permute-start | bytes 3145736 | tf_op jit(solution)/shard_map/ppermute | solution.py:36
  1030.8 14.2 %collective-permute-start.10 = (bf16[512,1024]{1,0:T(8,128)(2,1)S(1)}, bf16[512,1024]{1,0:T(8,128)(2,1)S(1)}, u32[]{:S(2)}, u32[]{:S(2)}) collective-permute-start(bf16[512,1024]{1,0:T(8,128)(2,1)S(1)} %collective-permute-done.9), channel_id=1, source_target_pairs={{0,1},{1,2},{2,3},{3,0},{4,5},{5,6},{6,7},{7,4},{8,9},{9,10},{10,1... | collective-permute-start | bytes 3145736 | tf_op jit(solution)/shard_map/ppermute | solution.py:36
  1045.0 59.6 %collective-permute-start.11 = (bf16[512,1024]{1,0:T(8,128)(2,1)S(1)}, bf16[512,1024]{1,0:T(8,128)(2,1)}, u32[]{:S(2)}, u32[]{:S(2)}) collective-permute-start(bf16[512,1024]{1,0:T(8,128)(2,1)S(1)} %collective-permute-done.10), channel_id=1, source_target_pairs={{0,1},{1,2},{2,3},{3,0},{4,5},{5,6},{6,7},{7,4},{8,9},{9,10},{10,1... | collective-permute-start | bytes 3145736 | tf_op jit(solution)/shard_map/ppermute | solution.py:36
  (1 other events, 13.4 us)
Sparse Core Ops, SparseCore 0:
  11.6 37.4 all-gather.11
  56.2 125.2 all-gather.9
  192.4 123.1 all-gather.13
  340.4 122.6 all-gather.15
  474.2 123.1 all-gather.17
  610.4 122.6 all-gather.19
  744.2 123.1 all-gather.21
  880.4 122.6 all-gather.23
  1016.6 123.8 all-gather.25
